TPU v7x, 128 devices: a whole 4x4x4 slice. The times are simulated.
128 devices in a mesh: dp: 16 (over z, x), expert: 8 (over y, core).
Axes of the slice: x: 4, y: 4, z: 4, core: 2. Of those that a mesh axis runs over, the one named last changes fastest.
Arguments:
- tokens: bfloat16 [16384, 2048], P(('dp', 'expert')), may hold values from -6 to 6
- cotangent: bfloat16 [16384, 2048], P(('dp', 'expert')), may hold values from -6 to 6
- expert_ids: int32 [16384, 2], P(('dp', 'expert')), may hold values from 0 to 7, all different within a row; in each aligned block of 128 rows (0 to 127, 128 to 255, ...) at most 36 rows name the same one
- route_share: float32 [16384], P(('dp', 'expert')), may hold values from 0.5 to 0.95
- gate_proj: bfloat16 [8, 7168, 2048], P('expert', 'dp'), may hold values from -0.125 to 0.125
- up_proj: bfloat16 [8, 7168, 2048], P('expert', 'dp'), may hold values from -0.125 to 0.125
- down_anchor: float32 [8, 7168, 2048], P('expert', 'dp'), may hold values from -0.12 to 0.12
- down_average: float32 [8, 7168, 2048], P('expert', 'dp'), may hold values from -0.12 to 0.12
- down_moment: float32 [8, 7168, 2048], P('expert', 'dp'), may hold values from 0.002 to 0.05
Outputs:
- new_anchor: float32 [8, 7168, 2048], P('expert', 'dp')
- new_average: float32 [8, 7168, 2048], P('expert', 'dp')
- new_moment: float32 [8, 7168, 2048], P('expert', 'dp')
Inputs may be any that keep to these rules, and one draw needn't show every extreme that they name: `expert_ids`: the two ids of a token differ. The rows of one device name any expert at most 36 times, and in every draw some device names some expert exactly 36 times.
All inputs are finite; a program needn't handle non-finite values.
Results may differ from a plain program's by a relative error of at most 0.0043.
Values may be sent and summed in bfloat16 or wider, within the bound.
No kernel may reach another device: no remote copies, remote signals or barrier semaphores. Data moves between devices by JAX's collectives and lax.ppermute only.
A program may use at most 192 MiB of HBM per device.

v0:
```python
import jax
import jax.numpy as jnp
from jax import lax
from jax.sharding import PartitionSpec as P

FF = 7168
TOPK = 2
beta_one = 0.9
beta_two = 0.95
learn_rate = 0.05
decay_rate = 0.1
step_count = 4.0
epsilon = 1e-08


def expert_terms(pieces, weight_gate, weight_up):
    rows_in, gated_rows = pieces
    gate_act = lax.dot_general(
        rows_in, weight_gate, (((1,), (1,)), ((), ())), preferred_element_type=jnp.float32
    )
    up_act = lax.dot_general(
        rows_in, weight_up, (((1,), (1,)), ((), ())), preferred_element_type=jnp.float32
    )
    hidden = (jax.nn.silu(gate_act) * up_act).astype(jnp.bfloat16)
    return lax.dot_general(
        hidden, gated_rows, (((0,), (0,)), ((), ())), preferred_element_type=jnp.float32
    )


def shards(
    tokens,
    cotangent,
    expert_ids,
    route_share,
    gate_proj,
    up_proj,
    down_anchor,
    down_average,
    down_moment,
):
    experts_all = lax.axis_size("expert")
    tok_rows = tokens.shape[0]
    width = tokens.shape[1]
    capacity = tok_rows * TOPK // experts_all * 9 // 8
    slots = experts_all * capacity
    shares = jnp.stack([route_share, 1.0 - route_share], axis=1)
    expert_range = jnp.arange(experts_all, dtype=jnp.int32)
    flat_ids = expert_ids.reshape(-1)
    onehot_routes = (flat_ids[:, None] == expert_range[None, :]).astype(jnp.int32)
    earlier = jnp.cumsum(onehot_routes, axis=0) - onehot_routes
    slot_of = jnp.sum(earlier * onehot_routes, axis=1)
    target = (flat_ids * capacity + slot_of).reshape(tok_rows, TOPK)
    slot_range = jnp.arange(slots, dtype=jnp.int32)
    placed = target[None, :, :] == slot_range[:, None, None]
    picker = jnp.sum(placed.astype(jnp.float32), axis=2).astype(jnp.bfloat16)
    slot_share = jnp.sum(jnp.where(placed, shares[None, :, :], 0.0), axis=(1, 2))
    send_rows = jnp.dot(picker, tokens, preferred_element_type=jnp.float32).astype(jnp.bfloat16)
    send_grad = (
        slot_share[:, None] * jnp.dot(picker, cotangent, preferred_element_type=jnp.float32)
    ).astype(jnp.bfloat16)
    weight_gate = gate_proj[0]
    weight_up = up_proj[0]
    arrived = (
        lax.all_to_all(
            send_rows.reshape(experts_all, capacity, width),
            "expert",
            split_axis=0,
            concat_axis=0,
            tiled=True,
        ),
        lax.all_to_all(
            send_grad.reshape(experts_all, capacity, width),
            "expert",
            split_axis=0,
            concat_axis=0,
            tiled=True,
        ),
    )
    rows_here = arrived[0].reshape(slots, width)
    grad_here = arrived[1].reshape(slots, width)
    gradient = expert_terms(
        (
            lax.all_gather(rows_here, "dp", axis=0, tiled=True),
            lax.all_gather(grad_here, "dp", axis=0, tiled=True),
        ),
        weight_gate,
        weight_up,
    )
    gradient = gradient[None] * FF ** (-0.5)
    bias_two = 1.0 - beta_two**step_count
    eval_point = (1.0 - beta_one) * down_anchor + beta_one * down_average
    second_moment = beta_two * down_moment + (1.0 - beta_two) * gradient * gradient
    update_dir = gradient / (jnp.sqrt(second_moment / bias_two) + epsilon) + decay_rate * eval_point
    new_anchor = down_anchor - learn_rate * update_dir
    new_average = (1.0 - 1.0 / step_count) * down_average + 1.0 / step_count * new_anchor
    return (new_anchor, new_average, second_moment)


def solution(mesh):
    placed = (
        P(("dp", "expert"), None),
        P(("dp", "expert"), None),
        P(("dp", "expert"), None),
        P(("dp", "expert")),
        P("expert", "dp", None),
        P("expert", "dp", None),
        P("expert", "dp", None),
        P("expert", "dp", None),
        P("expert", "dp", None),
    )
    return jax.shard_map(
        shards,
        mesh=mesh,
        in_specs=placed,
        out_specs=(P("expert", "dp", None), P("expert", "dp", None), P("expert", "dp", None)),
        check_vma=False,
    )
```

profile of v0, /device:TPU:1, one launch (start us, length us, event | category | flops | bytes accessed | tf_op | source)
XLA Modules:
  0.0 330.5 jit_solution(17586150212628106540)
XLA Ops:
  7.2 0.0 copy-start
  7.2 0.0 all-gather.3.cloned.1.call-start
  7.2 0.9 copy.24
  8.1 0.1 eq.42
  8.3 0.1 eq.38
  8.4 0.7 subtract_bitcast_fusion
  9.1 0.6 reduce-window.6
  9.7 0.2 slice_reduce_fusion
  9.9 0.1 fusion.11
  10.0 0.1 reduce_sum.30
  10.2 0.1 copy.26
  10.2 0.7 multiply_add_fusion.1
  10.9 0.7 pad_maximum_fusion
  11.6 0.2 select_reduce_fusion
  11.7 2.5 convolution_convert_fusion
  14.2 1.4 reshape.48
  15.6 23.6 %all_to_all.10 = bf16[8,36,2048]{2,1,0:T(8,128)(2,1)} all-to-all(bf16[8,36,2048]{2,1,0:T(8,128)(2,1)S(1)} %reshape.48), channel_id=1, replica_groups=mesh['dp'=16,'expert'=8] {'expert'}, dimensions={0} | all-to-all | bytes 2359296 | tf_op jit(solution)/shard_map/all_to_all | solution.py:64
  39.2 0.0 copy-start.1
  39.2 2.3 reshape.49
  41.5 0.0 all-gather.3.cloned.1.call-update
  41.5 0.0 all-gather.5.cloned.1.call-start
  41.6 0.0 copy-done.1
  41.6 1.5 fusion.4
  43.1 1.4 reshape.50
  44.5 21.9 %all_to_all.11 = bf16[8,36,2048]{2,1,0:T(8,128)(2,1)} all-to-all(bf16[8,36,2048]{2,1,0:T(8,128)(2,1)S(1)} %reshape.50), channel_id=1, replica_groups=mesh['dp'=16,'expert'=8] {'expert'}, dimensions={0} | all-to-all | bytes 2359296 | tf_op jit(solution)/shard_map/all_to_all | solution.py:71
  66.4 2.2 reshape.51
  68.6 0.0 all-gather.5.cloned.1.call-update
  68.6 95.7 %all-gather.3.cloned.1.call-done = bf16[4608,2048]{1,0:T(8,128)(2,1)} async-done(((bf16[288,2048]{1,0:T(8,128)(2,1)}), bf16[4608,2048]{1,0:T(8,128)(2,1)}) %all-gather.3.cloned.1.call-update) | async-done | bytes 18874384 | tf_op jit(solution)/shard_map/all_gather | solution.py:83
  164.3 15.2 %fusion.6 = f32[4608,448]{0,1:T(8,128)} fusion(bf16[4608,2048]{1,0:T(8,128)(2,1)} %all-gather.3.cloned.1.call-done, bf16[1,448,2048]{2,1,0:T(8,128)(2,1)} %param.13), kind=kOutput, calls=%fused_computation.12 | convolution fusion | flops 8455716864 | bytes 28966912 | tf_op jit(solution)/shard_map/dot_general | solution.py:18
  179.5 109.2 %all-gather.5.cloned.1.call-done = bf16[4608,2048]{1,0:T(8,128)(2,1)} async-done(((bf16[288,2048]{1,0:T(8,128)(2,1)}), bf16[4608,2048]{1,0:T(8,128)(2,1)}) %all-gather.5.cloned.1.call-update) | async-done | bytes 18874384 | tf_op jit(solution)/shard_map/all_gather | solution.py:84
  288.7 0.0 copy-done
  288.7 34.9 %multiply_add_fusion = (f32[1,448,2048]{2,1,0:T(8,128)}, f32[1,448,2048]{2,1,0:T(8,128)}, f32[1,448,2048]{2,1,0:T(8,128)}) fusion(f32[1,448,2048]{2,1,0:T(8,128)} %param.16, f32[1,448,2048]{2,1,0:T(8,128)} %param.15, f32[1,448,2048]{2,1,0:T(8,128)} %param.17, bf16[4608,2048]{1,0:T(8,128)(2,1)} %all-gather.5.cloned.1.call-done, ...), kind=kOutput, calls=%fused_computation.7 | convolution fusion | flops 16940335104 | bytes 69861376 | tf_op jit(solution)/shard_map/dot_general | solution.py:25
  (3 shorter events, 0.0 us)
Async XLA Ops:
  7.2 281.5 %copy-start = (bf16[1,448,2048]{2,1,0:T(8,128)(2,1)S(1)}, bf16[1,448,2048]{2,1,0:T(8,128)(2,1)}, u32[]{:S(2)}) copy-start(bf16[1,448,2048]{2,1,0:T(8,128)(2,1)} %param.14) | copy-start | bytes 5505028
  7.2 157.1 %all-gather.3.cloned.1.call-start = ((), (), s32[]{:S(2)}) async-start(), calls=%async_computation.2 | async-start | bytes 20054016 | tf_op jit(solution)/shard_map/all_gather | solution.py:83
  39.2 2.4 copy-start.1
  41.5 247.1 %all-gather.5.cloned.1.call-start = ((), (), s32[]{:S(2)}) async-start(), calls=%async_computation.3 | async-start | bytes 20054016 | tf_op jit(solution)/shard_map/all_gather | solution.py:84
Sparse Core Ops, SparseCore 0:
  41.7 122.6 all-gather.2
  167.0 121.6 all-gather.4
where the time goes:
time: 331 us; the launch traced here: 330 us
  waiting for transfers between devices  205 us (62%)
  matrix products  54.1 us (16%)
  blocking collectives  45.5 us (14%)
  between operations  14.1 us (4%)
  local copies, waits for them, and re-layouts  8.88 us (3%)
    all_gather x1, waiting for transfers between devices, shards(): lax.all_gather(grad_here, 'dp', axis=0, tiled=True)  109 us
    all_gather x1, waiting for transfers between devices, shards(): lax.all_gather(rows_here, 'dp', axis=0, tiled=True)  95.7 us
    dot_general x1, matrix products, expert_terms(): lax.dot_general(hidden, gated_rows, (((0,), (0,)), ((), ())), preferred_e...  34.9 us
    all_to_all x1, blocking collectives, shards(): lax.all_to_all(send_rows.reshape(experts_all, capacity, width), 'expert',...  23.6 us
    all_to_all x1, blocking collectives, shards(): lax.all_to_all(send_grad.reshape(experts_all, capacity, width), 'expert',...  21.9 us
    dot_general x1, matrix products, expert_terms(): lax.dot_general(rows_in, weight_gate, (((1,), (1,)), ((), ())), preferred...  15.2 us
  transfers between devices with their start and end apart: 2, of which 2 were waited for; matrix products, arithmetic and copies ran while one was open for 6% of the time, Pallas kernels for 0%

commit v1 on v0

--- a/solution.py
+++ b/solution.py
@@ -11,6 +11,19 @@
 decay_rate = 0.1
 step_count = 4.0
 epsilon = 1e-08
+
+
+def ring_gather(x, axis, dim):
+    ways = lax.axis_size(axis)
+    up = [(d, (d + 1) % ways) for d in range(ways)]
+    down = [(d, (d - 1) % ways) for d in range(ways)]
+    earlier, later = ([x], [x])
+    for _ in range(ways // 2):
+        earlier.append(lax.ppermute(earlier[-1], axis, up))
+    for _ in range((ways - 1) // 2):
+        later.append(lax.ppermute(later[-1], axis, down))
+    line = jnp.concatenate([*earlier[::-1], *later[1:]], axis=dim)
+    return jnp.roll(line, (lax.axis_index(axis) - ways // 2) * x.shape[dim], axis=dim)
 
 
 def expert_terms(pieces, weight_gate, weight_up):
@@ -79,10 +92,7 @@
     rows_here = arrived[0].reshape(slots, width)
     grad_here = arrived[1].reshape(slots, width)
     gradient = expert_terms(
-        (
-            lax.all_gather(rows_here, "dp", axis=0, tiled=True),
-            lax.all_gather(grad_here, "dp", axis=0, tiled=True),
-        ),
+        (lax.all_gather(rows_here, "dp", axis=0, tiled=True), ring_gather(grad_here, "dp", 0)),
         weight_gate,
         weight_up,
     )

time: 331 us -> 476 us (1.44); the launches traced: 330 us -> 467 us
  local copies, waits for them, and re-layouts: 8.88 us -> 61.7 us
  waiting for transfers between devices: 205 us -> 252 us
  starting transfers between devices: 0.08 us -> 35.7 us
    ppermute x0 -> x15, waiting for transfers between devices: none -> 252 us  [the longest x8 252 us: ring_gather(): earlier.append(lax.ppermute(earlier[-1], axis, up))]
    all_gather x1 -> x0, waiting for transfers between devices: 109 us -> none  [shards(): lax.all_gather(grad_here, 'dp', axis=0, tiled=True)]
    all_gather x1, waiting for transfers between devices: 95.7 us -> 0.01 us  [shards(): lax.all_gather(rows_here, 'dp', axis=0, tiled=True)]
    unnamed x5 -> x66, local copies, waits for them, and re-layouts: 0.92 us -> 53.4 us
    ppermute x0 -> x15, starting transfers between devices: none -> 35.7 us  [the longest x7 34.4 us: ring_gather(): later.append(lax.ppermute(later[-1], axis, down))]
  transfers between devices with their start and end apart: 2 -> 16, of which waited for: 2 -> 8; matrix products, arithmetic and copies ran while one was open for 6% -> 12% of each run, Pallas kernels for 0% -> 0%
where the time goes in v1:
time: 476 us; the launch traced here: 467 us
  waiting for transfers between devices  252 us (53%)
  local copies, waits for them, and re-layouts  61.7 us (13%)
  matrix products  55.4 us (12%)
  blocking collectives  45.5 us (10%)
  starting transfers between devices  35.7 us (8%)
  between operations  14.2 us (3%)
    ppermute x8, waiting for transfers between devices, ring_gather(): earlier.append(lax.ppermute(earlier[-1], axis, up))  252 us
    unnamed x66, local copies, waits for them, and re-layouts  53.4 us
    dot_general x1, matrix products, expert_terms(): lax.dot_general(hidden, gated_rows, (((0,), (0,)), ((), ())), preferred_e...  35.3 us
    ppermute x7, starting transfers between devices, ring_gather(): later.append(lax.ppermute(later[-1], axis, down))  34.4 us
    all_to_all x1, blocking collectives, shards(): lax.all_to_all(send_rows.reshape(experts_all, capacity, width), 'expert',...  23.6 us
    all_to_all x1, blocking collectives, shards(): lax.all_to_all(send_grad.reshape(experts_all, capacity, width), 'expert',...  21.9 us
    dot_general x1, matrix products, expert_terms(): lax.dot_general(rows_in, weight_gate, (((1,), (1,)), ((), ())), preferred...  15.1 us
  transfers between devices with their start and end apart: 16, of which 8 were waited for; matrix products, arithmetic and copies ran while one was open for 12% of the time, Pallas kernels for 0%

profile of v1, /device:TPU:1, one launch (start us, length us, event | category | flops | bytes accessed | tf_op | source)
XLA Modules:
  0.0 467.5 jit_solution(18371666901626123693)
XLA Ops:
  11.8 2.5 convolution_convert_fusion
  15.6 23.6 %all_to_all.10 = bf16[8,36,2048]{2,1,0:T(8,128)(2,1)} all-to-all(bf16[8,36,2048]{2,1,0:T(8,128)(2,1)S(1)} %reshape.48), channel_id=1, replica_groups=mesh['dp'=16,'expert'=8] {'expert'}, dimensions={0} | all-to-all | bytes 2359296 | tf_op jit(solution)/shard_map/all_to_all | solution.py:77
  41.5 2.5 fusion.6
  45.4 21.9 %all_to_all.11 = bf16[8,36,2048]{2,1,0:T(8,128)(2,1)} all-to-all(bf16[8,36,2048]{2,1,0:T(8,128)(2,1)S(1)} %reshape.50), channel_id=1, replica_groups=mesh['dp'=16,'expert'=8] {'expert'}, dimensions={0} | all-to-all | bytes 2359296 | tf_op jit(solution)/shard_map/all_to_all | solution.py:84
  70.1 43.5 %collective-permute-done = bf16[288,2048]{1,0:T(8,128)(2,1)S(1)} collective-permute-done((bf16[288,2048]{1,0:T(8,128)(2,1)S(1)}, bf16[288,2048]{1,0:T(8,128)(2,1)S(1)}, u32[]{:S(2)}, u32[]{:S(2)}) %collective-permute-start) | collective-permute-done | bytes 1179680 | tf_op jit(solution)/shard_map/ppermute | solution.py:22
  113.6 4.8 %collective-permute-start.8 = (bf16[288,2048]{1,0:T(8,128)(2,1)S(1)}, bf16[288,2048]{1,0:T(8,128)(2,1)S(1)}, u32[]{:S(2)}, u32[]{:S(2)}) collective-permute-start(bf16[288,2048]{1,0:T(8,128)(2,1)S(1)} %reshape.51), channel_id=1, source_target_pairs={{0,120},{8,0},{16,8},{24,16},{32,24},{40,32},{48,40},{56,48},{64,5... | collective-permute-start | bytes 3538952 | tf_op jit(solution)/shard_map/ppermute | solution.py:24
  118.3 51.3 %collective-permute-done.1 = bf16[288,2048]{1,0:T(8,128)(2,1)S(1)} collective-permute-done((bf16[288,2048]{1,0:T(8,128)(2,1)S(1)}, bf16[288,2048]{1,0:T(8,128)(2,1)S(1)}, u32[]{:S(2)}, u32[]{:S(2)}) %collective-permute-start.1) | collective-permute-done | bytes 1179680 | tf_op jit(solution)/shard_map/ppermute | solution.py:22
  169.7 4.8 %collective-permute-start.9 = (bf16[288,2048]{1,0:T(8,128)(2,1)S(1)}, bf16[288,2048]{1,0:T(8,128)(2,1)S(1)}, u32[]{:S(2)}, u32[]{:S(2)}) collective-permute-start(bf16[288,2048]{1,0:T(8,128)(2,1)S(1)} %collective-permute-done.8), channel_id=1, source_target_pairs={{0,120},{8,0},{16,8},{24,16},{32,24},{40,32},{48,40},{56,48},{64,5... | collective-permute-start | bytes 3538952 | tf_op jit(solution)/shard_map/ppermute | solution.py:24
  174.5 51.0 %collective-permute-done.2 = bf16[288,2048]{1,0:T(8,128)(2,1)S(1)} collective-permute-done((bf16[288,2048]{1,0:T(8,128)(2,1)S(1)}, bf16[288,2048]{1,0:T(8,128)(2,1)S(1)}, u32[]{:S(2)}, u32[]{:S(2)}) %collective-permute-start.2) | collective-permute-done | bytes 1179680 | tf_op jit(solution)/shard_map/ppermute | solution.py:22
  225.6 4.8 %collective-permute-start.10 = (bf16[288,2048]{1,0:T(8,128)(2,1)S(1)}, bf16[288,2048]{1,0:T(8,128)(2,1)S(1)}, u32[]{:S(2)}, u32[]{:S(2)}) collective-permute-start(bf16[288,2048]{1,0:T(8,128)(2,1)S(1)} %collective-permute-done.9), channel_id=1, source_target_pairs={{0,120},{8,0},{16,8},{24,16},{32,24},{40,32},{48,40},{56,48},{64,5... | collective-permute-start | bytes 3538952 | tf_op jit(solution)/shard_map/ppermute | solution.py:24
  230.4 23.0 %collective-permute-done.3 = bf16[288,2048]{1,0:T(8,128)(2,1)S(1)} collective-permute-done((bf16[288,2048]{1,0:T(8,128)(2,1)S(1)}, bf16[288,2048]{1,0:T(8,128)(2,1)S(1)}, u32[]{:S(2)}, u32[]{:S(2)}) %collective-permute-start.3) | collective-permute-done | bytes 1179680 | tf_op jit(solution)/shard_map/ppermute | solution.py:22
  253.5 4.8 %collective-permute-start.11 = (bf16[288,2048]{1,0:T(8,128)(2,1)S(1)}, bf16[288,2048]{1,0:T(8,128)(2,1)S(1)}, u32[]{:S(2)}, u32[]{:S(2)}) collective-permute-start(bf16[288,2048]{1,0:T(8,128)(2,1)S(1)} %collective-permute-done.10), channel_id=1, source_target_pairs={{0,120},{8,0},{16,8},{24,16},{32,24},{40,32},{48,40},{56,48},{64,5... | collective-permute-start | bytes 3538952 | tf_op jit(solution)/shard_map/ppermute | solution.py:24
  258.3 22.3 %collective-permute-done.4 = bf16[288,2048]{1,0:T(8,128)(2,1)} collective-permute-done((bf16[288,2048]{1,0:T(8,128)(2,1)S(1)}, bf16[288,2048]{1,0:T(8,128)(2,1)}, u32[]{:S(2)}, u32[]{:S(2)}) %collective-permute-start.4) | collective-permute-done | bytes 1179680 | tf_op jit(solution)/shard_map/ppermute | solution.py:22
  281.6 4.8 %collective-permute-start.12 = (bf16[288,2048]{1,0:T(8,128)(2,1)S(1)}, bf16[288,2048]{1,0:T(8,128)(2,1)}, u32[]{:S(2)}, u32[]{:S(2)}) collective-permute-start(bf16[288,2048]{1,0:T(8,128)(2,1)S(1)} %collective-permute-done.11), channel_id=1, source_target_pairs={{0,120},{8,0},{16,8},{24,16},{32,24},{40,32},{48,40},{56,48},{64,5... | collective-permute-start | bytes 3538952 | tf_op jit(solution)/shard_map/ppermute | solution.py:24
  286.4 20.7 %collective-permute-done.5 = bf16[288,2048]{1,0:T(8,128)(2,1)} collective-permute-done((bf16[288,2048]{1,0:T(8,128)(2,1)}, bf16[288,2048]{1,0:T(8,128)(2,1)}, u32[]{:S(2)}, u32[]{:S(2)}) %collective-permute-start.5) | collective-permute-done | bytes 1179680 | tf_op jit(solution)/shard_map/ppermute | solution.py:22
  307.1 5.3 %collective-permute-start.13 = (bf16[288,2048]{1,0:T(8,128)(2,1)}, bf16[288,2048]{1,0:T(8,128)(2,1)}, u32[]{:S(2)}, u32[]{:S(2)}) collective-permute-start(bf16[288,2048]{1,0:T(8,128)(2,1)} %collective-permute-done.12), channel_id=1, source_target_pairs={{0,120},{8,0},{16,8},{24,16},{32,24},{40,32},{48,40},{56,48},{64,5... | collective-permute-start | bytes 3538952 | tf_op jit(solution)/shard_map/ppermute | solution.py:24
  312.4 20.3 %collective-permute-done.6 = bf16[288,2048]{1,0:T(8,128)(2,1)} collective-permute-done((bf16[288,2048]{1,0:T(8,128)(2,1)}, bf16[288,2048]{1,0:T(8,128)(2,1)}, u32[]{:S(2)}, u32[]{:S(2)}) %collective-permute-start.6) | collective-permute-done | bytes 1179680 | tf_op jit(solution)/shard_map/ppermute | solution.py:22
  332.8 5.0 %collective-permute-start.14 = (bf16[288,2048]{1,0:T(8,128)(2,1)}, bf16[288,2048]{1,0:T(8,128)(2,1)S(1)}, u32[]{:S(2)}, u32[]{:S(2)}) collective-permute-start(bf16[288,2048]{1,0:T(8,128)(2,1)} %collective-permute-done.13), channel_id=1, source_target_pairs={{0,120},{8,0},{16,8},{24,16},{32,24},{40,32},{48,40},{56,48},{64,5... | collective-permute-start | bytes 3538952 | tf_op jit(solution)/shard_map/ppermute | solution.py:24
  337.8 19.8 %collective-permute-done.7 = bf16[288,2048]{1,0:T(8,128)(2,1)} collective-permute-done((bf16[288,2048]{1,0:T(8,128)(2,1)}, bf16[288,2048]{1,0:T(8,128)(2,1)}, u32[]{:S(2)}, u32[]{:S(2)}) %collective-permute-start.7) | collective-permute-done | bytes 1179680 | tf_op jit(solution)/shard_map/ppermute | solution.py:22
  357.5 2.4 constant_dynamic-update-slice_fusion.31
  362.4 2.5 constant_dynamic-update-slice_fusion.29
  364.9 2.5 constant_dynamic-update-slice_fusion.28
  377.9 2.4 constant_dynamic-update-slice_fusion.18
  380.3 2.4 constant_dynamic-update-slice_fusion.17
  383.9 2.4 constant_dynamic-update-slice_fusion.15
  386.4 2.4 constant_dynamic-update-slice_fusion.14
  388.8 2.5 constant_dynamic-update-slice_fusion.13
  391.2 2.4 constant_dynamic-update-slice_fusion.12
  404.1 2.4 constant_dynamic-update-slice_fusion.2
  406.6 2.4 constant_dynamic-update-slice_fusion.1
  410.2 15.1 %fusion.10 = f32[4608,448]{0,1:T(8,128)} fusion(bf16[4608,2048]{1,0:T(8,128)(2,1)} %all-gather.2.cloned.1.call-done, bf16[1,448,2048]{2,1,0:T(8,128)(2,1)} %param.13), kind=kOutput, calls=%fused_computation.14 | convolution fusion | flops 8455716864 | bytes 28966912 | tf_op jit(solution)/shard_map/dot_general | solution.py:31
  425.3 35.3 %multiply_add_fusion = (f32[1,448,2048]{2,1,0:T(8,128)}, f32[1,448,2048]{2,1,0:T(8,128)}, f32[1,448,2048]{2,1,0:T(8,128)}) fusion(f32[1,448,2048]{2,1,0:T(8,128)} %param.16, f32[1,448,2048]{2,1,0:T(8,128)} %param.15, f32[1,448,2048]{2,1,0:T(8,128)} %param.17, bf16[9216,2048]{1,0:T(8,128)(2,1)} %constant_dynamic-update-slice_fusion, s32[]{:T(128)S(6)} %select_n.19, ...), kind=kOutput, calls=%fused_computation.9 | convolution fusion | flops 16940335104 | bytes 69861376 | tf_op jit(solution)/shard_map/dot_general | solution.py:38
  (92 shorter events, 39.1 us)
Async XLA Ops:
  7.2 418.1 %copy-start = (bf16[1,448,2048]{2,1,0:T(8,128)(2,1)S(1)}, bf16[1,448,2048]{2,1,0:T(8,128)(2,1)}, u32[]{:S(2)}) copy-start(bf16[1,448,2048]{2,1,0:T(8,128)(2,1)} %param.14) | copy-start | bytes 5505028
  7.2 403.0 %all-gather.2.cloned.1.call-start = ((), (), s32[]{:S(2)}) async-start(), calls=%async_computation.2 | async-start | bytes 20054016 | tf_op jit(solution)/shard_map/all_gather | solution.py:95
  68.8 44.8 %collective-permute-start = (bf16[288,2048]{1,0:T(8,128)(2,1)S(1)}, bf16[288,2048]{1,0:T(8,128)(2,1)S(1)}, u32[]{:S(2)}, u32[]{:S(2)}) collective-permute-start(bf16[288,2048]{1,0:T(8,128)(2,1)S(1)} %reshape.51), channel_id=1, source_target_pairs={{0,8},{8,16},{16,24},{24,32},{32,40},{40,48},{48,56},{56,64},{64,7... | collective-permute-start | bytes 3538952 | tf_op jit(solution)/shard_map/ppermute | solution.py:22
  113.6 56.1 %copy-start.1 = (bf16[288,2048]{1,0:T(8,128)(2,1)}, bf16[288,2048]{1,0:T(8,128)(2,1)S(1)}, u32[]{:S(2)}) copy-start(bf16[288,2048]{1,0:T(8,128)(2,1)S(1)} %collective-permute-done) | copy-start | bytes 3538948
  113.6 56.1 %collective-permute-start.1 = (bf16[288,2048]{1,0:T(8,128)(2,1)S(1)}, bf16[288,2048]{1,0:T(8,128)(2,1)S(1)}, u32[]{:S(2)}, u32[]{:S(2)}) collective-permute-start(bf16[288,2048]{1,0:T(8,128)(2,1)S(1)} %collective-permute-done), channel_id=1, source_target_pairs={{0,8},{8,16},{16,24},{24,32},{32,40},{40,48},{48,56},{56,64},{64,7... | collective-permute-start | bytes 3538952 | tf_op jit(solution)/shard_map/ppermute | solution.py:22
  113.6 56.1 %collective-permute-start.8 = (bf16[288,2048]{1,0:T(8,128)(2,1)S(1)}, bf16[288,2048]{1,0:T(8,128)(2,1)S(1)}, u32[]{:S(2)}, u32[]{:S(2)}) collective-permute-start(bf16[288,2048]{1,0:T(8,128)(2,1)S(1)} %reshape.51), channel_id=1, source_target_pairs={{0,120},{8,0},{16,8},{24,16},{32,24},{40,32},{48,40},{56,48},{64,5... | collective-permute-start | bytes 3538952 | tf_op jit(solution)/shard_map/ppermute | solution.py:24
  169.7 55.9 %copy-start.5 = (bf16[288,2048]{1,0:T(8,128)(2,1)}, bf16[288,2048]{1,0:T(8,128)(2,1)S(1)}, u32[]{:S(2)}) copy-start(bf16[288,2048]{1,0:T(8,128)(2,1)S(1)} %collective-permute-done.1) | copy-start | bytes 3538948
  169.7 55.9 %collective-permute-start.2 = (bf16[288,2048]{1,0:T(8,128)(2,1)S(1)}, bf16[288,2048]{1,0:T(8,128)(2,1)S(1)}, u32[]{:S(2)}, u32[]{:S(2)}) collective-permute-start(bf16[288,2048]{1,0:T(8,128)(2,1)S(1)} %collective-permute-done.1), channel_id=1, source_target_pairs={{0,8},{8,16},{16,24},{24,32},{32,40},{40,48},{48,56},{56,64},{64,7... | collective-permute-start | bytes 3538952 | tf_op jit(solution)/shard_map/ppermute | solution.py:22
  169.7 4.8 %copy-start.3 = (bf16[288,2048]{1,0:T(8,128)(2,1)}, bf16[288,2048]{1,0:T(8,128)(2,1)S(1)}, u32[]{:S(2)}) copy-start(bf16[288,2048]{1,0:T(8,128)(2,1)S(1)} %collective-permute-done.8) | copy-start | bytes 3538948
  169.7 55.8 %collective-permute-start.9 = (bf16[288,2048]{1,0:T(8,128)(2,1)S(1)}, bf16[288,2048]{1,0:T(8,128)(2,1)S(1)}, u32[]{:S(2)}, u32[]{:S(2)}) collective-permute-start(bf16[288,2048]{1,0:T(8,128)(2,1)S(1)} %collective-permute-done.8), channel_id=1, source_target_pairs={{0,120},{8,0},{16,8},{24,16},{32,24},{40,32},{48,40},{56,48},{64,5... | collective-permute-start | bytes 3538952 | tf_op jit(solution)/shard_map/ppermute | solution.py:24
  225.5 27.9 %copy-start.9 = (bf16[288,2048]{1,0:T(8,128)(2,1)}, bf16[288,2048]{1,0:T(8,128)(2,1)S(1)}, u32[]{:S(2)}) copy-start(bf16[288,2048]{1,0:T(8,128)(2,1)S(1)} %collective-permute-done.2) | copy-start | bytes 3538948
  225.5 27.9 %collective-permute-start.3 = (bf16[288,2048]{1,0:T(8,128)(2,1)S(1)}, bf16[288,2048]{1,0:T(8,128)(2,1)S(1)}, u32[]{:S(2)}, u32[]{:S(2)}) collective-permute-start(bf16[288,2048]{1,0:T(8,128)(2,1)S(1)} %collective-permute-done.2), channel_id=1, source_target_pairs={{0,8},{8,16},{16,24},{24,32},{32,40},{40,48},{48,56},{56,64},{64,7... | collective-permute-start | bytes 3538952 | tf_op jit(solution)/shard_map/ppermute | solution.py:22
  225.6 4.8 %copy-start.7 = (bf16[288,2048]{1,0:T(8,128)(2,1)}, bf16[288,2048]{1,0:T(8,128)(2,1)S(1)}, u32[]{:S(2)}) copy-start(bf16[288,2048]{1,0:T(8,128)(2,1)S(1)} %collective-permute-done.9) | copy-start | bytes 3538948
  225.6 27.9 %collective-permute-start.10 = (bf16[288,2048]{1,0:T(8,128)(2,1)S(1)}, bf16[288,2048]{1,0:T(8,128)(2,1)S(1)}, u32[]{:S(2)}, u32[]{:S(2)}) collective-permute-start(bf16[288,2048]{1,0:T(8,128)(2,1)S(1)} %collective-permute-done.9), channel_id=1, source_target_pairs={{0,120},{8,0},{16,8},{24,16},{32,24},{40,32},{48,40},{56,48},{64,5... | collective-permute-start | bytes 3538952 | tf_op jit(solution)/shard_map/ppermute | solution.py:24
  253.4 53.7 %copy-start.15 = (bf16[288,2048]{1,0:T(8,128)(2,1)}, bf16[288,2048]{1,0:T(8,128)(2,1)S(1)}, u32[]{:S(2)}) copy-start(bf16[288,2048]{1,0:T(8,128)(2,1)S(1)} %collective-permute-done.3) | copy-start | bytes 3538948
  253.4 27.2 %collective-permute-start.4 = (bf16[288,2048]{1,0:T(8,128)(2,1)S(1)}, bf16[288,2048]{1,0:T(8,128)(2,1)}, u32[]{:S(2)}, u32[]{:S(2)}) collective-permute-start(bf16[288,2048]{1,0:T(8,128)(2,1)S(1)} %collective-permute-done.3), channel_id=1, source_target_pairs={{0,8},{8,16},{16,24},{24,32},{32,40},{40,48},{48,56},{56,64},{64,7... | collective-permute-start | bytes 3538952 | tf_op jit(solution)/shard_map/ppermute | solution.py:22
  253.5 4.8 %copy-start.11 = (bf16[288,2048]{1,0:T(8,128)(2,1)}, bf16[288,2048]{1,0:T(8,128)(2,1)S(1)}, u32[]{:S(2)}) copy-start(bf16[288,2048]{1,0:T(8,128)(2,1)S(1)} %collective-permute-done.10) | copy-start | bytes 3538948
  253.5 27.1 %collective-permute-start.11 = (bf16[288,2048]{1,0:T(8,128)(2,1)S(1)}, bf16[288,2048]{1,0:T(8,128)(2,1)S(1)}, u32[]{:S(2)}, u32[]{:S(2)}) collective-permute-start(bf16[288,2048]{1,0:T(8,128)(2,1)S(1)} %collective-permute-done.10), channel_id=1, source_target_pairs={{0,120},{8,0},{16,8},{24,16},{32,24},{40,32},{48,40},{56,48},{64,5... | collective-permute-start | bytes 3538952 | tf_op jit(solution)/shard_map/ppermute | solution.py:24
  280.6 26.5 %collective-permute-start.5 = (bf16[288,2048]{1,0:T(8,128)(2,1)}, bf16[288,2048]{1,0:T(8,128)(2,1)}, u32[]{:S(2)}, u32[]{:S(2)}) collective-permute-start(bf16[288,2048]{1,0:T(8,128)(2,1)} %collective-permute-done.4), channel_id=1, source_target_pairs={{0,8},{8,16},{16,24},{24,32},{32,40},{40,48},{48,56},{56,64},{64,7... | collective-permute-start | bytes 3538952 | tf_op jit(solution)/shard_map/ppermute | solution.py:22
  281.6 25.5 %collective-permute-start.12 = (bf16[288,2048]{1,0:T(8,128)(2,1)S(1)}, bf16[288,2048]{1,0:T(8,128)(2,1)}, u32[]{:S(2)}, u32[]{:S(2)}) collective-permute-start(bf16[288,2048]{1,0:T(8,128)(2,1)S(1)} %collective-permute-done.11), channel_id=1, source_target_pairs={{0,120},{8,0},{16,8},{24,16},{32,24},{40,32},{48,40},{56,48},{64,5... | collective-permute-start | bytes 3538952 | tf_op jit(solution)/shard_map/ppermute | solution.py:24
  307.1 25.6 %collective-permute-start.6 = (bf16[288,2048]{1,0:T(8,128)(2,1)}, bf16[288,2048]{1,0:T(8,128)(2,1)}, u32[]{:S(2)}, u32[]{:S(2)}) collective-permute-start(bf16[288,2048]{1,0:T(8,128)(2,1)} %collective-permute-done.5), channel_id=1, source_target_pairs={{0,8},{8,16},{16,24},{24,32},{32,40},{40,48},{48,56},{56,64},{64,7... | collective-permute-start | bytes 3538952 | tf_op jit(solution)/shard_map/ppermute | solution.py:22
  307.1 25.7 %collective-permute-start.13 = (bf16[288,2048]{1,0:T(8,128)(2,1)}, bf16[288,2048]{1,0:T(8,128)(2,1)}, u32[]{:S(2)}, u32[]{:S(2)}) collective-permute-start(bf16[288,2048]{1,0:T(8,128)(2,1)} %collective-permute-done.12), channel_id=1, source_target_pairs={{0,120},{8,0},{16,8},{24,16},{32,24},{40,32},{48,40},{56,48},{64,5... | collective-permute-start | bytes 3538952 | tf_op jit(solution)/shard_map/ppermute | solution.py:24
  332.7 24.8 %collective-permute-start.7 = (bf16[288,2048]{1,0:T(8,128)(2,1)}, bf16[288,2048]{1,0:T(8,128)(2,1)}, u32[]{:S(2)}, u32[]{:S(2)}) collective-permute-start(bf16[288,2048]{1,0:T(8,128)(2,1)} %collective-permute-done.6), channel_id=1, source_target_pairs={{0,8},{8,16},{16,24},{24,32},{32,40},{40,48},{48,56},{56,64},{64,7... | collective-permute-start | bytes 3538952 | tf_op jit(solution)/shard_map/ppermute | solution.py:22
  332.7 34.7 %copy-start.16 = (bf16[288,2048]{1,0:T(8,128)(2,1)S(1)}, bf16[288,2048]{1,0:T(8,128)(2,1)}, u32[]{:S(2)}) copy-start(bf16[288,2048]{1,0:T(8,128)(2,1)} %copy-done.15) | copy-start | bytes 3538948
  332.8 35.9 %copy-start.10 = (bf16[288,2048]{1,0:T(8,128)(2,1)S(1)}, bf16[288,2048]{1,0:T(8,128)(2,1)}, u32[]{:S(2)}) copy-start(bf16[288,2048]{1,0:T(8,128)(2,1)} %copy-done.9) | copy-start | bytes 3538948
  332.8 37.0 %copy-start.6 = (bf16[288,2048]{1,0:T(8,128)(2,1)S(1)}, bf16[288,2048]{1,0:T(8,128)(2,1)}, u32[]{:S(2)}) copy-start(bf16[288,2048]{1,0:T(8,128)(2,1)} %copy-done.5) | copy-start | bytes 3538948
  332.8 38.2 %copy-start.2 = (bf16[288,2048]{1,0:T(8,128)(2,1)S(1)}, bf16[288,2048]{1,0:T(8,128)(2,1)}, u32[]{:S(2)}) copy-start(bf16[288,2048]{1,0:T(8,128)(2,1)} %copy-done.1) | copy-start | bytes 3538948
  332.8 50.0 %collective-permute-start.14 = (bf16[288,2048]{1,0:T(8,128)(2,1)}, bf16[288,2048]{1,0:T(8,128)(2,1)S(1)}, u32[]{:S(2)}, u32[]{:S(2)}) collective-permute-start(bf16[288,2048]{1,0:T(8,128)(2,1)} %collective-permute-done.13), channel_id=1, source_target_pairs={{0,120},{8,0},{16,8},{24,16},{32,24},{40,32},{48,40},{56,48},{64,5... | collective-permute-start | bytes 3538952 | tf_op jit(solution)/shard_map/ppermute | solution.py:24
  362.4 10.9 %copy-start.4 = (bf16[288,2048]{1,0:T(8,128)(2,1)S(1)}, bf16[288,2048]{1,0:T(8,128)(2,1)}, u32[]{:S(2)}) copy-start(bf16[288,2048]{1,0:T(8,128)(2,1)} %copy-done.3) | copy-start | bytes 3538948
  364.9 9.5 %copy-start.8 = (bf16[288,2048]{1,0:T(8,128)(2,1)S(1)}, bf16[288,2048]{1,0:T(8,128)(2,1)}, u32[]{:S(2)}) copy-start(bf16[288,2048]{1,0:T(8,128)(2,1)} %copy-done.7) | copy-start | bytes 3538948
  367.5 8.2 %copy-start.12 = (bf16[288,2048]{1,0:T(8,128)(2,1)S(1)}, bf16[288,2048]{1,0:T(8,128)(2,1)}, u32[]{:S(2)}) copy-start(bf16[288,2048]{1,0:T(8,128)(2,1)} %copy-done.11) | copy-start | bytes 3538948
  368.6 8.2 %copy-start.14 = (bf16[288,2048]{1,0:T(8,128)(2,1)S(1)}, bf16[288,2048]{1,0:T(8,128)(2,1)}, u32[]{:S(2)}) copy-start(bf16[288,2048]{1,0:T(8,128)(2,1)} %copy-done.13) | copy-start | bytes 3538948
  (1 other events, 1.0 us)
Sparse Core Ops, SparseCore 0:
  41.6 188.7 all-gather.1
